TPU v7x, 32 devices: a whole 2x2x4 slice. The times are simulated.
32 devices in a mesh: tenant: 2 (over y), ctx: 2 (over x), head: 8 (over z, core).
Axes of the slice: x: 2, y: 2, z: 4, core: 2. Of those that a mesh axis runs over, the one named last changes fastest.
Arguments:
- tokens: bfloat16 [1024, 4608], P(('tenant', 'ctx'), 'head'), parts along dimension 0, may hold values from -6 to 6
- query_frozen_matrix: bfloat16 [4608, 2048], P('ctx', 'head'), may hold values from -0.09375 to 0.09375
- key_weight: bfloat16 [4608, 1024], P('ctx', 'head'), may hold values from -0.09375 to 0.09375
- value_frozen_matrix: bfloat16 [4608, 1024], P('ctx', 'head'), may hold values from -0.09375 to 0.09375
- query_down: bfloat16 [9216, 16], P('tenant'), parts along dimension 0, may hold values from -0.09375 to 0.09375
- query_adapter_expand: bfloat16 [32, 2048], P('tenant', 'head'), parts along dimension 0, may hold values from -1.5 to 1.5
- value_down: bfloat16 [9216, 16], P('tenant'), parts along dimension 0, may hold values from -0.09375 to 0.09375
- value_adapter_expand: bfloat16 [32, 1024], P('tenant', 'head'), parts along dimension 0, may hold values from -1.5 to 1.5
- block_order: int32 [8], P('tenant'), parts along dimension 0, may hold values from 0 to 3, each once
- doc_starts: int32 [24], P('tenant'), parts along dimension 0, may hold values from 0 to 511, as said below
- prompt_of: int32 [24], P('tenant'), parts along dimension 0, may hold values from 0 to 11, as said below
Outputs:
- attended: bfloat16 [1024, 2048], P(('tenant', 'ctx'), 'head'), parts along dimension 0
There are 2 independent parts, one for each index of `tenant`. A program takes and returns all parts, laid end to end along the dimension named above; an argument that names none is the same for every part. Nothing has to cross between parts.
Inputs may be any that keep to these rules, and one draw needn't show every extreme that they name: `doc_starts`: strictly increasing with first entry 0; the segments come in 4 groups of three: a prompt, a chosen and a rejected response. `prompt_of`: for segment j = 3k it is j; for j = 3k + 1 it is 3k; for j = 3k + 2 it is 3k or j. `block_order`: each of 0 to 3 once.
All inputs are finite; a program needn't handle non-finite values.
Results may differ from a plain program's by a relative error of at most 0.012.
Values may be sent and summed in bfloat16 or wider, within the bound.
No kernel may reach another device: no remote copies, remote signals or barrier semaphores. Data moves between devices by JAX's collectives and lax.ppermute only.
A program may use at most 64 MiB of HBM per device.

v0:
```python
import math
import jax
import jax.numpy as jnp
from jax import lax
from jax.sharding import PartitionSpec as P

HD = 128
softcap_limit = 50.0
query_scale = 144.0 ** (-0.5)
adapter_scaling = 2.0
rope_base = 10000.0


def row_meta(row_ids, block_order, doc_starts, prompt_of, block_len, sequence_len):
    block_count = block_order.shape[0]
    block_id = row_ids // block_len
    one_hot = block_id[:, None] == jnp.arange(block_count, dtype=jnp.int32)[None, :]
    ordered = jnp.sum(jnp.where(one_hot, block_order[None, :], 0), axis=1)
    places = ordered * block_len + row_ids % block_len
    segment = jnp.sum((doc_starts[None, :] <= places[:, None]).astype(jnp.int32), axis=1) - 1
    seg_ids = jnp.arange(doc_starts.shape[0], dtype=jnp.int32)
    selected = segment[:, None] == seg_ids[None, :]
    prompt_seg = jnp.sum(jnp.where(selected, prompt_of[None, :], 0), axis=1)
    own_start = jnp.sum(jnp.where(selected, doc_starts[None, :], 0), axis=1)
    next_starts = jnp.concatenate([doc_starts[1:], jnp.full((1,), sequence_len, jnp.int32)])
    prompt_sel = prompt_seg[:, None] == seg_ids[None, :]
    prompt_len = jnp.sum(jnp.where(prompt_sel, (next_starts - doc_starts)[None, :], 0), axis=1)
    rotary_pos = places - own_start + jnp.where(prompt_seg != segment, prompt_len, 0)
    return (places, segment, prompt_seg, rotary_pos)


def rotate(values_in, rotary_pos):
    width_half = values_in.shape[-1] // 2
    frequency = jnp.exp(
        jnp.arange(width_half, dtype=jnp.float32)
        * (-2.0 * math.log(rope_base) / values_in.shape[-1])
    )
    angles = rotary_pos.astype(jnp.float32)[:, None] * frequency[None, :]
    cosine = jnp.concatenate([jnp.cos(angles), jnp.cos(angles)], axis=-1)[:, None, :]
    sine_part = jnp.concatenate([jnp.sin(angles), jnp.sin(angles)], axis=-1)[:, None, :]
    rotated = jnp.concatenate([-values_in[..., width_half:], values_in[..., :width_half]], axis=-1)
    return values_in * cosine + rotated * sine_part


def visible_mask(query_info, key_info):
    same_doc = (key_info[1][None, :] == query_info[1][:, None]) & (
        key_info[0][None, :] <= query_info[0][:, None]
    )
    from_prompt = (key_info[1][None, :] == query_info[2][:, None]) & (
        query_info[2] != query_info[1]
    )[:, None]
    return same_doc | from_prompt


def local(
    tokens,
    query_frozen_matrix,
    key_weight,
    value_frozen_matrix,
    query_down,
    query_adapter_expand,
    value_down,
    value_adapter_expand,
    block_order,
    doc_starts,
    prompt_of,
):
    tok_rows = tokens.shape[0]
    cycle_size = lax.axis_size("ctx")
    device = lax.axis_index("ctx")
    sequence_len = tok_rows * cycle_size
    block_len = tok_rows // 2
    full_tokens = lax.all_gather(tokens, "head", axis=1, tiled=True)

    def add_rows(weight_part):
        return jnp.dot(full_tokens, weight_part, preferred_element_type=jnp.float32)

    frozen_query_output = add_rows(lax.all_gather(query_frozen_matrix, "ctx", axis=0, tiled=True))
    key_base = add_rows(lax.all_gather(key_weight, "ctx", axis=0, tiled=True))
    frozen_value_output = add_rows(lax.all_gather(value_frozen_matrix, "ctx", axis=0, tiled=True))
    own_ids = device * tok_rows + jnp.arange(tok_rows, dtype=jnp.int32)
    own_info = row_meta(own_ids, block_order, doc_starts, prompt_of, block_len, sequence_len)
    local_heads = query_frozen_matrix.shape[1] // HD
    local_kv = key_weight.shape[1] // HD
    per_kv = local_heads // local_kv
    query_adapter_hidden = jnp.dot(
        full_tokens, query_down, preferred_element_type=jnp.float32
    ).astype(jnp.bfloat16)
    query_states = frozen_query_output + adapter_scaling * jnp.dot(
        query_adapter_hidden, query_adapter_expand, preferred_element_type=jnp.float32
    )
    query_states = (
        rotate(query_states.reshape(tok_rows, local_heads, HD), own_info[3]) * query_scale
    ).astype(jnp.bfloat16)
    query_heads = query_states.reshape(tok_rows, local_kv, per_kv, HD)
    key_proj = (
        rotate(key_base.reshape(tok_rows, local_kv, HD), own_info[3])
        .astype(jnp.bfloat16)
        .reshape(tok_rows, local_kv * HD)
    )
    value_adapter_hidden = jnp.dot(
        full_tokens, value_down, preferred_element_type=jnp.float32
    ).astype(jnp.bfloat16)
    value_projected = (
        frozen_value_output
        + adapter_scaling
        * jnp.dot(value_adapter_hidden, value_adapter_expand, preferred_element_type=jnp.float32)
    ).astype(jnp.bfloat16)
    pieces = (
        lax.all_gather(key_proj, "ctx", axis=0, tiled=True),
        lax.all_gather(value_projected, "ctx", axis=0, tiled=True),
    )
    key_ids = jnp.arange(pieces[0].shape[0], dtype=jnp.int32)
    key_block = pieces[0]
    value_block = pieces[1]
    key_info = row_meta(key_ids, block_order, doc_starts, prompt_of, block_len, sequence_len)
    visible = visible_mask(own_info, key_info)
    key_heads = key_block.reshape(key_block.shape[0], local_kv, HD)
    value_heads = value_block.reshape(value_block.shape[0], local_kv, HD)
    scores = jnp.einsum(
        "tkgd,skd->kgts", query_heads, key_heads, preferred_element_type=jnp.float32
    )
    capped = softcap_limit * jnp.tanh(scores / softcap_limit)
    unnorm = jnp.where(visible[None, None], jnp.exp(capped), jnp.zeros_like(capped))
    denominator = jnp.sum(unnorm, axis=-1)
    numerator = jnp.einsum(
        "kgts,skd->tkgd",
        unnorm.astype(jnp.bfloat16),
        value_heads,
        preferred_element_type=jnp.float32,
    )
    numerator, denominator = (numerator, denominator)
    attended = numerator / jnp.transpose(denominator, (2, 0, 1))[..., None]
    return attended.reshape(tok_rows, local_heads * HD).astype(jnp.bfloat16)


def solution(mesh):
    in_specs = (
        P(("tenant", "ctx"), "head"),
        P("ctx", "head"),
        P("ctx", "head"),
        P("ctx", "head"),
        P("tenant", None),
        P("tenant", "head"),
        P("tenant", None),
        P("tenant", "head"),
        P("tenant"),
        P("tenant"),
        P("tenant"),
    )
    out_specs = P(("tenant", "ctx"), "head")
    return jax.shard_map(local, mesh=mesh, in_specs=in_specs, out_specs=out_specs, check_vma=False)
```

profile of v0, /device:TPU:0, one launch (start us, length us, event | category | flops | bytes accessed | tf_op | source)
XLA Modules:
  0.0 143.6 jit_solution(536576771758366168)
XLA Ops:
  6.5 0.0 all-gather.9.cloned.1.call-start
  6.6 0.7 all-gather.9.cloned.1.call-update
  7.3 0.0 all-gather.5.cloned.1.call-start
  7.3 0.7 all-gather.5.cloned.1.call-update
  8.0 0.0 all-gather.11.cloned.1.call-start
  8.1 0.7 all-gather.11.cloned.1.call-update
  8.8 0.0 all-gather.7.cloned.1.call-start
  8.8 0.5 all-gather.7.cloned.1.call-update
  9.4 0.1 slice.15
  9.5 0.1 select_reduce_fusion.4
  9.6 0.1 convert_reduce_fusion.1
  9.7 0.1 select_reduce_fusion.3
  9.7 0.1 convert_reduce_fusion
  9.8 0.1 add_subtract_fusion
  9.9 0.1 select_reduce_fusion.1
  10.0 0.1 select_reduce_fusion
  10.1 0.3 multiply_cosine_fusion
  10.4 0.2 and_or_fusion
  10.7 23.7 %all-gather.9.cloned.1.call-done = bf16[4608,128]{1,0:T(8,128)(2,1)} async-done(((bf16[2304,128]{1,0:T(8,128)(2,1)}), bf16[4608,128]{1,0:T(8,128)(2,1)}) %all-gather.9.cloned.1.call-update) | async-done | bytes 1179664 | tf_op jit(solution)/shard_map/all_gather | solution.py:79
  34.4 33.1 %all-gather.5.cloned.1.call-done = bf16[256,4608]{0,1:T(8,128)(2,1)} async-done(((bf16[256,576]{0,1:T(8,128)(2,1)}), bf16[256,4608]{0,1:T(8,128)(2,1)}) %all-gather.5.cloned.1.call-update) | async-done | bytes 2359312 | tf_op jit(solution)/shard_map/all_gather | solution.py:73
  67.5 2.7 %fusion.30 = f32[256,128]{0,1:T(8,128)S(1)} fusion(bf16[256,4608]{0,1:T(8,128)(2,1)} %all-gather.5.cloned.1.call-done, bf16[4608,128]{1,0:T(8,128)(2,1)} %all-gather.9.cloned.1.call-done), kind=kOutput, calls=%fused_computation.76 | convolution fusion | flops 301989888 | bytes 3670016 | tf_op jit(solution)/shard_map/dot_general | solution.py:76
  70.4 4.9 %all_gather.22 = bf16[512,128]{0,1:T(8,128)(2,1)S(1)} all-gather(bf16[256,128]{0,1:T(8,128)(2,1)S(1)} %get-tuple-element.13), channel_id=1, replica_groups=mesh['tenant'=2,'ctx'=2,'head'=8] {'ctx'}, dimensions={0}, use_global_device_ids=true | all-gather | bytes 196608 | tf_op jit(solution)/shard_map/all_gather | solution.py:110
  75.3 1.0 convolution_multiply_fusion.1
  76.3 28.1 %all-gather.11.cloned.1.call-done = bf16[4608,256]{1,0:T(8,128)(2,1)} async-done(((bf16[2304,256]{1,0:T(8,128)(2,1)}), bf16[4608,256]{1,0:T(8,128)(2,1)}) %all-gather.11.cloned.1.call-update) | async-done | bytes 2359312 | tf_op jit(solution)/shard_map/all_gather | solution.py:78
  104.4 2.7 %convolution_add_fusion = f32[256,256]{0,1:T(8,128)S(1)} fusion(f32[256,256]{0,1:T(8,128)S(1)} %convolution_multiply_fusion.1, bf16[256,4608]{0,1:T(8,128)(2,1)S(1)} %copy-done.4, bf16[4608,256]{1,0:T(8,128)(2,1)} %all-gather.11.cloned.1.call-done), kind=kOutput, calls=%fused_computation.7 | convolution fusion | flops 604045312 | bytes 5242880 | tf_op jit(solution)/shard_map/dot_general | solution.py:76
  107.1 2.5 %convolution_multiply_fusion.2 = f32[256,128]{0,1:T(8,128)} fusion(bf16[16,128]{1,0:T(8,128)(2,1)} %param.18, bf16[256,4608]{0,1:T(8,128)(2,1)S(1)} %copy-done.4, bf16[4608,16]{0,1:T(8,128)(2,1)} %param.17), kind=kOutput, calls=%fused_computation.10 | convolution fusion | flops 38834176 | bytes 2641920 | tf_op jit(solution)/shard_map/dot_general | solution.py:107
  109.7 18.9 %all-gather.7.cloned.1.call-done = bf16[4608,128]{1,0:T(8,128)(2,1)} async-done(((bf16[2304,128]{1,0:T(8,128)(2,1)}), bf16[4608,128]{1,0:T(8,128)(2,1)}) %all-gather.7.cloned.1.call-update) | async-done | bytes 1179664 | tf_op jit(solution)/shard_map/all_gather | solution.py:80
  128.6 1.9 %fusion.5 = bf16[256,128]{0,1:T(8,128)(2,1)S(1)} fusion(f32[256,128]{0,1:T(8,128)} %convolution_multiply_fusion.2, bf16[256,4608]{0,1:T(8,128)(2,1)S(1)} %copy-done.4, bf16[4608,128]{1,0:T(8,128)(2,1)} %all-gather.7.cloned.1.call-done), kind=kOutput, calls=%fused_computation.11 | convolution fusion | flops 302055424 | bytes 3735552 | tf_op jit(solution)/shard_map/dot_general | solution.py:76
  130.5 4.9 %all_gather.20 = bf16[512,128]{0,1:T(8,128)(2,1)S(1)} all-gather(bf16[256,128]{0,1:T(8,128)(2,1)S(1)} %fusion.5), channel_id=1, replica_groups=mesh['tenant'=2,'ctx'=2,'head'=8] {'ctx'}, dimensions={0}, use_global_device_ids=true | all-gather | bytes 196608 | tf_op jit(solution)/shard_map/all_gather | solution.py:111
  135.5 0.5 fusion.29
  136.0 0.2 fusion.7
  136.3 0.8 copy.19
  (25 shorter events, 0.2 us)
Async XLA Ops:
  6.5 68.8 %copy-start = (bf16[4608,16]{0,1:T(8,128)(2,1)S(1)}, bf16[4608,16]{0,1:T(8,128)(2,1)}, u32[]{:S(2)}) copy-start(bf16[4608,16]{0,1:T(8,128)(2,1)} %param.15) | copy-start | bytes 442372
  6.5 2.8 %copy-start.1 = (s32[12]{0:T(128)S(1)}, s32[12]{0:T(128)}, u32[]{:S(2)}) copy-start(s32[12]{0:T(128)} %param.20) | copy-start | bytes 148
  6.5 2.9 %copy-start.2 = (s32[4]{0:T(128)S(1)}, s32[4]{0:T(128)}, u32[]{:S(2)}) copy-start(s32[4]{0:T(128)} %param.19) | copy-start | bytes 52
  6.5 3.4 %copy-start.3 = (s32[12]{0:T(128)S(1)}, s32[12]{0:T(128)}, u32[]{:S(2)}) copy-start(s32[12]{0:T(128)} %param.21) | copy-start | bytes 148
  6.5 27.9 %all-gather.9.cloned.1.call-start = ((), (), s32[]{:S(2)}) async-start(), calls=%async_computation.2 | async-start | bytes 1769472 | tf_op jit(solution)/shard_map/all_gather | solution.py:79
  7.3 60.3 %all-gather.5.cloned.1.call-start = ((), (), s32[]{:S(2)}) async-start(), calls=%async_computation | async-start | bytes 2654208 | tf_op jit(solution)/shard_map/all_gather | solution.py:73
  8.0 96.4 %all-gather.11.cloned.1.call-start = ((), (), s32[]{:S(2)}) async-start(), calls=%async_computation.3 | async-start | bytes 3538944 | tf_op jit(solution)/shard_map/all_gather | solution.py:78
  8.8 119.8 %all-gather.7.cloned.1.call-start = ((), (), s32[]{:S(2)}) async-start(), calls=%async_computation.1 | async-start | bytes 1769472 | tf_op jit(solution)/shard_map/all_gather | solution.py:80
  10.7 64.6 %copy-start.5 = (bf16[16,256]{1,0:T(8,128)(2,1)S(1)}, bf16[16,256]{1,0:T(8,128)(2,1)}, u32[]{:S(2)}) copy-start(bf16[16,256]{1,0:T(8,128)(2,1)} %param.16) | copy-start | bytes 24580
  67.5 7.8 %copy-start.4 = (bf16[256,4608]{0,1:T(8,128)(2,1)S(1)}, bf16[256,4608]{0,1:T(8,128)(2,1)}, u32[]{:S(2)}) copy-start(bf16[256,4608]{0,1:T(8,128)(2,1)} %all-gather.5.cloned.1.call-done) | copy-start | bytes 7077892
Sparse Core Ops, SparseCore 0:
  8.9 25.4 all-gather.8
  36.1 31.4 all-gather.4
  69.1 35.2 all-gather.10
  105.8 22.7 all-gather.6
where the time goes:
time: 144 us
  waiting for transfers between devices  106 us (74%)
  between operations  13.3 us (9%)
  matrix products  11.6 us (8%)
  blocking collectives  9.87 us (7%)
    all_gather x1, waiting for transfers between devices, local(): full_tokens = lax.all_gather(tokens, 'head', axis=1, tiled=True)  33.1 us
    all_gather x1, waiting for transfers between devices, local(): lax.all_gather(query_frozen_matrix, 'ctx', axis=0, tiled=True)  28.1 us
    all_gather x1, waiting for transfers between devices, local(): key_base = add_rows(lax.all_gather(key_weight, 'ctx', axis=0, tiled=True))  23.7 us
    all_gather x1, waiting for transfers between devices, local(): lax.all_gather(value_frozen_matrix, 'ctx', axis=0, tiled=True)  18.9 us
    dot_general x3, matrix products, add_rows(): return jnp.dot(full_tokens, weight_part, preferred_element_type=jnp.float32)  7.33 us
    all_gather x1, blocking collectives, local(): lax.all_gather(key_proj, 'ctx', axis=0, tiled=True)  4.93 us
    all_gather x1, blocking collectives, local(): lax.all_gather(value_projected, 'ctx', axis=0, tiled=True)  4.93 us
  transfers between devices with their start and end apart: 4, of which 4 were waited for; matrix products, arithmetic and copies ran while one was open for 7% of the time, Pallas kernels for 0%

commit v1 on v0

--- a/solution.py
+++ b/solution.py
@@ -70,7 +70,12 @@
     device = lax.axis_index("ctx")
     sequence_len = tok_rows * cycle_size
     block_len = tok_rows // 2
-    full_tokens = lax.all_gather(tokens, "head", axis=1, tiled=True)
+    ring = [tokens]
+    for hop in range(7):
+        ring.append(lax.ppermute(ring[-1], "head", [(dev, (dev + 1) % 8) for dev in range(8)]))
+    full_tokens = jnp.roll(
+        jnp.concatenate(ring[::-1], axis=1), (lax.axis_index("head") + 1) * ring[0].shape[1], axis=1
+    )
 
     def add_rows(weight_part):
         return jnp.dot(full_tokens, weight_part, preferred_element_type=jnp.float32)

time: 144 us -> 113 us (0.78)
  waiting for transfers between devices: 106 us -> 51.8 us
  local copies, waits for them, and re-layouts: 0.86 us -> 13.3 us
  other arithmetic: 1.36 us -> 5.3 us
  matrix products: 11.6 us -> 15.4 us
  blocking collectives: 9.87 us -> 13.2 us
    ppermute x0 -> x7, waiting for transfers between devices: none -> 50.2 us  [local(): lax.ppermute(ring[-1], 'head', [(dev, (dev + 1) % 8) for dev in range(8)])]
    all_gather x1 -> x0, waiting for transfers between devices: 33.1 us -> none  [local(): full_tokens = lax.all_gather(tokens, 'head', axis=1, tiled=True)]
    all_gather x1, waiting for transfers between devices: 28.1 us -> 0.02 us  [local(): lax.all_gather(query_frozen_matrix, 'ctx', axis=0, tiled=True)]
    all_gather x1, waiting for transfers between devices: 23.7 us -> 0.01 us  [local(): key_base = add_rows(lax.all_gather(key_weight, 'ctx', axis=0, tiled=True))]
    all_gather x1, waiting for transfers between devices: 18.9 us -> 0.02 us  [local(): lax.all_gather(value_frozen_matrix, 'ctx', axis=0, tiled=True)]
    unnamed x12 -> x25, local copies, waits for them, and re-layouts: 0.03 us -> 11.1 us
    dot_general x3, matrix products: 7.33 us -> 9.36 us  [add_rows(): return jnp.dot(full_tokens, weight_part, preferred_element_type=jnp.float32)]
    all_gather x1, blocking collectives: 4.93 us -> 6.7 us  [local(): lax.all_gather(value_projected, 'ctx', axis=0, tiled=True)]
  transfers between devices with their start and end apart: 4 -> 10, of which waited for: 4 -> 7; matrix products, arithmetic and copies ran while one was open for 7% -> 25% of each run, Pallas kernels for 0% -> 0%
where the time goes in v1:
time: 113 us
  waiting for transfers between devices  51.8 us (46%)
  matrix products  15.4 us (14%)
  local copies, waits for them, and re-layouts  13.3 us (12%)
  between operations  13.3 us (12%)
  blocking collectives  13.2 us (12%)
  other arithmetic  5.3 us (5%)
    ppermute x7, waiting for transfers between devices, local(): lax.ppermute(ring[-1], 'head', [(dev, (dev + 1) % 8) for dev in range(8)])  50.2 us
    unnamed x25, local copies, waits for them, and re-layouts  11.1 us
    dot_general x3, matrix products, add_rows(): return jnp.dot(full_tokens, weight_part, preferred_element_type=jnp.float32)  9.36 us
    all_gather x1, blocking collectives, local(): lax.all_gather(value_projected, 'ctx', axis=0, tiled=True)  6.7 us
    all_gather x1, blocking collectives, local(): lax.all_gather(key_proj, 'ctx', axis=0, tiled=True)  6.49 us
    dot_general x1, matrix products, local(): jnp.dot(query_adapter_hidden, query_adapter_expand, preferred_element_typ...  2.67 us
    dot_general x1, matrix products, local(): jnp.dot(value_adapter_hidden, value_adapter_expand, preferred_element_typ...  2.63 us
  transfers between devices with their start and end apart: 10, of which 7 were waited for; matrix products, arithmetic and copies ran while one was open for 25% of the time, Pallas kernels for 0%

profile of v1, /device:TPU:0, one launch (start us, length us, event | category | flops | bytes accessed | tf_op | source)
XLA Modules:
  0.0 112.9 jit_solution(1882307261535063923)
XLA Ops:
  9.5 0.7 select_reduce_fusion.4
  10.3 0.7 convert_reduce_fusion.1
  11.0 6.2 %collective-permute-done = bf16[256,576]{0,1:T(8,128)(2,1)S(1)} collective-permute-done((bf16[256,576]{0,1:T(8,128)(2,1)}, bf16[256,576]{0,1:T(8,128)(2,1)S(1)}, u32[]{:S(2)}, u32[]{:S(2)}) %collective-permute-start) | collective-permute-done | bytes 294944 | tf_op jit(solution)/shard_map/ppermute | solution.py:75
  17.3 0.8 select_reduce_fusion.1
  18.0 7.2 %collective-permute-done.1 = bf16[256,576]{0,1:T(8,128)(2,1)S(1)} collective-permute-done((bf16[256,576]{0,1:T(8,128)(2,1)S(1)}, bf16[256,576]{0,1:T(8,128)(2,1)S(1)}, u32[]{:S(2)}, u32[]{:S(2)}) %collective-permute-start.1) | collective-permute-done | bytes 294944 | tf_op jit(solution)/shard_map/ppermute | solution.py:75
  25.2 0.7 select_reduce_fusion.3
  25.9 7.2 %collective-permute-done.2 = bf16[256,576]{0,1:T(8,128)(2,1)S(1)} collective-permute-done((bf16[256,576]{0,1:T(8,128)(2,1)S(1)}, bf16[256,576]{0,1:T(8,128)(2,1)S(1)}, u32[]{:S(2)}, u32[]{:S(2)}) %collective-permute-start.2) | collective-permute-done | bytes 294944 | tf_op jit(solution)/shard_map/ppermute | solution.py:75
  33.1 0.7 convert_reduce_fusion
  34.6 6.5 %collective-permute-done.3 = bf16[256,576]{0,1:T(8,128)(2,1)S(1)} collective-permute-done((bf16[256,576]{0,1:T(8,128)(2,1)S(1)}, bf16[256,576]{0,1:T(8,128)(2,1)S(1)}, u32[]{:S(2)}, u32[]{:S(2)}) %collective-permute-start.3) | collective-permute-done | bytes 294944 | tf_op jit(solution)/shard_map/ppermute | solution.py:75
  41.2 7.8 %collective-permute-done.4 = bf16[256,576]{0,1:T(8,128)(2,1)S(1)} collective-permute-done((bf16[256,576]{0,1:T(8,128)(2,1)S(1)}, bf16[256,576]{0,1:T(8,128)(2,1)S(1)}, u32[]{:S(2)}, u32[]{:S(2)}) %collective-permute-start.4) | collective-permute-done | bytes 294944 | tf_op jit(solution)/shard_map/ppermute | solution.py:75
  49.4 7.6 %collective-permute-done.5 = bf16[256,576]{0,1:T(8,128)(2,1)S(1)} collective-permute-done((bf16[256,576]{0,1:T(8,128)(2,1)S(1)}, bf16[256,576]{0,1:T(8,128)(2,1)S(1)}, u32[]{:S(2)}, u32[]{:S(2)}) %collective-permute-start.5) | collective-permute-done | bytes 294944 | tf_op jit(solution)/shard_map/ppermute | solution.py:75
  57.3 7.7 %collective-permute-done.6 = bf16[256,576]{0,1:T(8,128)(2,1)S(1)} collective-permute-done((bf16[256,576]{0,1:T(8,128)(2,1)S(1)}, bf16[256,576]{0,1:T(8,128)(2,1)S(1)}, u32[]{:S(2)}, u32[]{:S(2)}) %collective-permute-start.6) | collective-permute-done | bytes 294944 | tf_op jit(solution)/shard_map/ppermute | solution.py:75
  64.9 0.7 constant_dynamic-update-slice_fusion.15
  65.7 0.7 constant_dynamic-update-slice_fusion.14
  67.1 0.7 constant_dynamic-update-slice_fusion.12
  67.9 0.7 constant_dynamic-update-slice_fusion.11
  68.6 0.7 constant_dynamic-update-slice_fusion.10
  70.1 0.8 constant_dynamic-update-slice_fusion.8
  70.8 0.7 constant_dynamic-update-slice_fusion.7
  71.6 0.7 constant_dynamic-update-slice_fusion.6
  72.3 0.7 constant_dynamic-update-slice_fusion.5
  73.0 0.7 constant_dynamic-update-slice_fusion.4
  74.5 0.8 constant_dynamic-update-slice_fusion.2
  76.0 0.8 constant_dynamic-update-slice_fusion
  76.8 2.6 %convolution_multiply_fusion.2 = f32[256,128]{0,1:T(8,128)S(1)} fusion(bf16[16,128]{1,0:T(8,128)(2,1)S(1)} %copy-done.4, bf16[4608,16]{0,1:T(8,128)(2,1)S(1)} %copy-done.2, bf16[256,9216]{0,1:T(8,128)(2,1)} %constant_dynamic-update-slice_fusion, s32[]{:T(128)S(6)} %select_n.89), kind=kOutput, calls=%fused_computation.20 | convolution fusion | flops 38834176 | bytes 2641924 | tf_op jit(solution)/shard_map/dot_general | solution.py:112
  79.4 2.9 %fusion.21 = bf16[256,128]{0,1:T(8,128)(2,1)S(1)} fusion(f32[256,128]{0,1:T(8,128)S(1)} %convolution_multiply_fusion.2, bf16[4608,128]{1,0:T(8,128)(2,1)} %all-gather.4.cloned.1.call-done, bf16[256,9216]{0,1:T(8,128)(2,1)} %constant_dynamic-update-slice_fusion, s32[]{:T(128)S(6)} %select_n.89), kind=kOutput, calls=%fused_computation.21 | convolution fusion | flops 302055424 | bytes 3735556 | tf_op jit(solution)/shard_map/dot_general | solution.py:81
  82.3 6.7 %all_gather.16 = bf16[512,128]{0,1:T(8,128)(2,1)S(1)} all-gather(bf16[256,128]{0,1:T(8,128)(2,1)S(1)} %fusion.21), channel_id=1, replica_groups=mesh['tenant'=2,'ctx'=2,'head'=8] {'ctx'}, dimensions={0}, use_global_device_ids=true | all-gather | bytes 196608 | tf_op jit(solution)/shard_map/all_gather | solution.py:116
  89.0 2.9 %fusion.9 = f32[256,128]{0,1:T(8,128)S(1)} fusion(bf16[4608,128]{1,0:T(8,128)(2,1)} %all-gather.6.cloned.1.call-done, bf16[256,9216]{0,1:T(8,128)(2,1)} %constant_dynamic-update-slice_fusion, s32[]{:T(128)S(6)} %select_n.89), kind=kOutput, calls=%fused_computation.10 | convolution fusion | flops 301989888 | bytes 3670020 | tf_op jit(solution)/shard_map/dot_general | solution.py:81
  91.9 6.5 %all_gather.18 = bf16[512,128]{0,1:T(8,128)(2,1)S(1)} all-gather(bf16[256,128]{0,1:T(8,128)(2,1)S(1)} %get-tuple-element.13), channel_id=1, replica_groups=mesh['tenant'=2,'ctx'=2,'head'=8] {'ctx'}, dimensions={0}, use_global_device_ids=true | all-gather | bytes 196608 | tf_op jit(solution)/shard_map/all_gather | solution.py:115
  98.4 2.7 %convolution_multiply_fusion.1 = f32[256,256]{0,1:T(8,128)S(1)} fusion(bf16[16,256]{1,0:T(8,128)(2,1)S(1)} %copy-done.3, bf16[4608,16]{0,1:T(8,128)(2,1)S(1)} %copy-done, bf16[256,9216]{0,1:T(8,128)(2,1)} %constant_dynamic-update-slice_fusion, s32[]{:T(128)S(6)} %select_n.89), kind=kOutput, calls=%fused_computation.18 | convolution fusion | flops 39915520 | bytes 2777092 | tf_op jit(solution)/shard_map/dot_general | solution.py:94
  101.1 3.6 %fusion.15 = f32[256,256]{0,1:T(8,128)S(1)} fusion(f32[256,256]{0,1:T(8,128)S(1)} %convolution_multiply_fusion.1, bf16[4608,256]{1,0:T(8,128)(2,1)} %all-gather.8.cloned.1.call-done, bf16[256,9216]{0,1:T(8,128)(2,1)} %constant_dynamic-update-slice_fusion, s32[]{:T(128)S(6)} %select_n.89), kind=kOutput, calls=%fused_computation.16 | convolution fusion | flops 604045312 | bytes 5242884 | tf_op jit(solution)/shard_map/dot_general | solution.py:81
  105.6 0.8 copy.19
  (50 shorter events, 8.2 us)
Async XLA Ops:
  6.5 91.9 %copy-start = (bf16[4608,16]{0,1:T(8,128)(2,1)S(1)}, bf16[4608,16]{0,1:T(8,128)(2,1)}, u32[]{:S(2)}) copy-start(bf16[4608,16]{0,1:T(8,128)(2,1)} %param.15) | copy-start | bytes 442372
  6.5 63.5 %copy-start.1 = (bf16[256,576]{0,1:T(8,128)(2,1)S(1)}, bf16[256,576]{0,1:T(8,128)(2,1)}, u32[]{:S(2)}) copy-start(bf16[256,576]{0,1:T(8,128)(2,1)} %param.11) | copy-start | bytes 884740
  6.5 72.9 %all-gather.4.cloned.1.call-start = ((), (), s32[]{:S(2)}) async-start(), calls=%async_computation | async-start | bytes 1769472 | tf_op jit(solution)/shard_map/all_gather | solution.py:85
  7.3 81.8 %all-gather.6.cloned.1.call-start = ((), (), s32[]{:S(2)}) async-start(), calls=%async_computation.1 | async-start | bytes 1769472 | tf_op jit(solution)/shard_map/all_gather | solution.py:84
  8.0 93.1 %all-gather.8.cloned.1.call-start = ((), (), s32[]{:S(2)}) async-start(), calls=%async_computation.2 | async-start | bytes 3538944 | tf_op jit(solution)/shard_map/all_gather | solution.py:83
  8.1 9.2 %collective-permute-start = (bf16[256,576]{0,1:T(8,128)(2,1)}, bf16[256,576]{0,1:T(8,128)(2,1)S(1)}, u32[]{:S(2)}, u32[]{:S(2)}) collective-permute-start(bf16[256,576]{0,1:T(8,128)(2,1)} %param.11), channel_id=1, source_target_pairs={{0,1},{1,2},{2,3},{3,4},{4,5},{5,6},{6,7},{7,0},{8,9},{9,10},{10,1... | collective-permute-start | bytes 884744 | tf_op jit(solution)/shard_map/ppermute | solution.py:75
  17.2 7.9 %collective-permute-start.1 = (bf16[256,576]{0,1:T(8,128)(2,1)S(1)}, bf16[256,576]{0,1:T(8,128)(2,1)S(1)}, u32[]{:S(2)}, u32[]{:S(2)}) collective-permute-start(bf16[256,576]{0,1:T(8,128)(2,1)S(1)} %collective-permute-done), channel_id=1, source_target_pairs={{0,1},{1,2},{2,3},{3,4},{4,5},{5,6},{6,7},{7,0},{8,9},{9,10},{10,1... | collective-permute-start | bytes 884744 | tf_op jit(solution)/shard_map/ppermute | solution.py:75
  25.2 7.9 %collective-permute-start.2 = (bf16[256,576]{0,1:T(8,128)(2,1)S(1)}, bf16[256,576]{0,1:T(8,128)(2,1)S(1)}, u32[]{:S(2)}, u32[]{:S(2)}) collective-permute-start(bf16[256,576]{0,1:T(8,128)(2,1)S(1)} %collective-permute-done.1), channel_id=1, source_target_pairs={{0,1},{1,2},{2,3},{3,4},{4,5},{5,6},{6,7},{7,0},{8,9},{9,10},{10,1... | collective-permute-start | bytes 884744 | tf_op jit(solution)/shard_map/ppermute | solution.py:75
  33.1 7.9 %collective-permute-start.3 = (bf16[256,576]{0,1:T(8,128)(2,1)S(1)}, bf16[256,576]{0,1:T(8,128)(2,1)S(1)}, u32[]{:S(2)}, u32[]{:S(2)}) collective-permute-start(bf16[256,576]{0,1:T(8,128)(2,1)S(1)} %collective-permute-done.2), channel_id=1, source_target_pairs={{0,1},{1,2},{2,3},{3,4},{4,5},{5,6},{6,7},{7,0},{8,9},{9,10},{10,1... | collective-permute-start | bytes 884744 | tf_op jit(solution)/shard_map/ppermute | solution.py:75
  41.1 7.9 %collective-permute-start.4 = (bf16[256,576]{0,1:T(8,128)(2,1)S(1)}, bf16[256,576]{0,1:T(8,128)(2,1)S(1)}, u32[]{:S(2)}, u32[]{:S(2)}) collective-permute-start(bf16[256,576]{0,1:T(8,128)(2,1)S(1)} %collective-permute-done.3), channel_id=1, source_target_pairs={{0,1},{1,2},{2,3},{3,4},{4,5},{5,6},{6,7},{7,0},{8,9},{9,10},{10,1... | collective-permute-start | bytes 884744 | tf_op jit(solution)/shard_map/ppermute | solution.py:75
  49.0 7.9 %collective-permute-start.5 = (bf16[256,576]{0,1:T(8,128)(2,1)S(1)}, bf16[256,576]{0,1:T(8,128)(2,1)S(1)}, u32[]{:S(2)}, u32[]{:S(2)}) collective-permute-start(bf16[256,576]{0,1:T(8,128)(2,1)S(1)} %collective-permute-done.4), channel_id=1, source_target_pairs={{0,1},{1,2},{2,3},{3,4},{4,5},{5,6},{6,7},{7,0},{8,9},{9,10},{10,1... | collective-permute-start | bytes 884744 | tf_op jit(solution)/shard_map/ppermute | solution.py:75
  57.0 7.9 %collective-permute-start.6 = (bf16[256,576]{0,1:T(8,128)(2,1)S(1)}, bf16[256,576]{0,1:T(8,128)(2,1)S(1)}, u32[]{:S(2)}, u32[]{:S(2)}) collective-permute-start(bf16[256,576]{0,1:T(8,128)(2,1)S(1)} %collective-permute-done.5), channel_id=1, source_target_pairs={{0,1},{1,2},{2,3},{3,4},{4,5},{5,6},{6,7},{7,0},{8,9},{9,10},{10,1... | collective-permute-start | bytes 884744 | tf_op jit(solution)/shard_map/ppermute | solution.py:75
  57.2 19.5 %copy-start.2 = (bf16[4608,16]{0,1:T(8,128)(2,1)S(1)}, bf16[4608,16]{0,1:T(8,128)(2,1)}, u32[]{:S(2)}) copy-start(bf16[4608,16]{0,1:T(8,128)(2,1)} %param.17) | copy-start | bytes 442372
  57.2 19.5 %copy-start.4 = (bf16[16,128]{1,0:T(8,128)(2,1)S(1)}, bf16[16,128]{1,0:T(8,128)(2,1)}, u32[]{:S(2)}) copy-start(bf16[16,128]{1,0:T(8,128)(2,1)} %param.18) | copy-start | bytes 12292
  79.4 19.1 %copy-start.3 = (bf16[16,256]{1,0:T(8,128)(2,1)S(1)}, bf16[16,256]{1,0:T(8,128)(2,1)}, u32[]{:S(2)}) copy-start(bf16[16,256]{1,0:T(8,128)(2,1)} %param.16) | copy-start | bytes 24580
Sparse Core Ops, SparseCore 0:
  8.9 25.4 all-gather.3
  35.9 22.7 all-gather.5
  60.3 38.8 all-gather.7
